TPU v7x, 32 devices: a whole 2x2x4 slice. The times are simulated.
32 devices in a mesh: gx: 8 (over y, x, core), gy: 4 (over z).
Axes of the slice: x: 2, y: 2, z: 4, core: 2. Of those that a mesh axis runs over, the one named last changes fastest.
Arguments:
- probes: float32 [16, 128, 128, 256], P(None, 'gx', 'gy'), may hold values from -6 to 6
- diffusivity: float32 [128, 128, 256], P('gx', 'gy'), may hold values from 0.5 to 2
- wind_speed: float32 [3], replicated, may hold values from 0.5 to 2
- sensor_cell: int32 [8, 4, 128], P('gx', 'gy'), may hold values from 0 to 131071
- sensor_owner: int32 [8, 4, 128, 1], P('gx', 'gy'), may hold values from 0 to 31; in each aligned block of 128 rows (0 to 127, 128 to 255, ..., all dimensions but the last counted through in order) at most 4 rows name the same one
- sensor_count: int32 [8, 4], P('gx', 'gy'), may hold values from 64 to 128
- goal_weight: float32 [8, 4, 128, 16], P('gx', 'gy'), may hold values from -0.6 to 0.6
Outputs:
- fields: float32 [16, 128, 128, 256], P(None, 'gx', 'gy')
- goal_block: float32 [512, 16], P(('gx', 'gy'))
- ritz_gram: float32 [16, 16], replicated
Inputs may be any that keep to these rules, and one draw needn't show every extreme that they name: `sensor_owner`: among the rows of one device, no owner is named more than 4 times, a bound that some block reaches.
All inputs are finite; a program needn't handle non-finite values.
Results may differ from a plain program's by a relative error of at most 0.0003.
Values sent between devices are 32-bit elements; how exact they have to be, the bound alone decides.
A program may use at most 192 MiB of HBM per device.

v0:
```python
import jax
import jax.numpy as jnp
from jax import lax
from jax.sharding import PartitionSpec as P

STEPS = 2
SWEEPS = 4
time_step = 2.0


def padded_2(cells, sides, width):
    for axis, dim in sides:
        count = lax.axis_size(axis)
        ends = count - 1
        head = lax.slice_in_dim(cells, 0, width, axis=dim)
        tail = lax.slice_in_dim(cells, cells.shape[dim] - width, cells.shape[dim], axis=dim)
        cells = jnp.concatenate(
            [
                lax.ppermute(tail, axis, [(i, (i + 1) % count) for i in range(ends)]),
                cells,
                lax.ppermute(head, axis, [((i + 1) % count, i) for i in range(ends)]),
            ],
            axis=dim,
        )
    return cells


def relax(padded, source, diffusion, wind_speed):
    centre = padded[..., 1:-1, 1:-1, :]
    widths = [(0, 0)] * (centre.ndim - 1) + [(1, 1)]
    zpadded = jnp.pad(centre, widths)
    beside = padded[..., 2:, 1:-1, :] + padded[..., :-2, 1:-1, :]
    beside = beside + padded[..., 1:-1, 2:, :] + padded[..., 1:-1, :-2, :]
    beside = beside + zpadded[..., 2:] + zpadded[..., :-2]
    upwind = (
        wind_speed[0] * padded[..., :-2, 1:-1, :]
        + wind_speed[1] * padded[..., 1:-1, :-2, :]
        + wind_speed[2] * zpadded[..., :-2]
    )
    diagonal = 1.0 + time_step * (6.0 * diffusion + wind_speed[0] + wind_speed[1] + wind_speed[2])
    updated = (source + time_step * (diffusion * beside + upwind)) / diagonal
    return jnp.where(diffusion > 0.0, updated, 0.0)


def body(probes, diffusivity, wind_speed, sensor_cell, sensor_owner, sensor_count, goal_weight):
    state_field = probes
    for step_index in range(STEPS):
        source = state_field
        for sweep_index in range(SWEEPS):
            padded = padded_2(state_field, (("gx", 1), ("gy", 2)), 1)
            state_field = relax(padded, source, diffusivity, wind_speed)
    probe_count = state_field.shape[0]
    sensor_rows = sensor_cell.shape[2]
    goal_count = goal_weight.shape[3]
    device_count = lax.axis_size("gx") * lax.axis_size("gy")
    capacity = max(2, (sensor_rows + device_count - 1) // device_count)
    flattened = state_field.reshape(probe_count, -1)
    readings = jnp.take(flattened, sensor_cell.reshape(-1), axis=1)
    row_index = jnp.arange(sensor_rows, dtype=jnp.int32)
    active = (row_index < sensor_count.reshape(())).astype(jnp.float32)
    readings = readings.T * active[:, None]
    weights = goal_weight.reshape(sensor_rows, goal_count)
    owners = sensor_owner.reshape(sensor_rows)
    earlier = (owners[None, :] == owners[:, None]) & (row_index[None, :] < row_index[:, None])
    slot_rank = jnp.sum(earlier.astype(jnp.int32), axis=1)
    slot_index = owners * capacity + slot_rank
    placing = (
        jnp.arange(device_count * capacity, dtype=jnp.int32)[:, None] == slot_index[None, :]
    ).astype(jnp.float32)
    payload = jnp.concatenate([readings, weights], axis=1)
    outgoing = jnp.dot(placing, payload, precision=lax.Precision.HIGHEST).reshape(
        device_count, capacity, probe_count + goal_count
    )
    received = lax.all_to_all(outgoing, ("gx", "gy"), split_axis=0, concat_axis=0, tiled=True)
    goal_block = jnp.einsum(
        "scj,scp->jp",
        received[..., probe_count:],
        received[..., :probe_count],
        precision=lax.Precision.HIGHEST,
    )
    ritz_gram = lax.psum(
        jnp.dot(goal_block.T, goal_block, precision=lax.Precision.HIGHEST), ("gx", "gy")
    )
    return (state_field, goal_block, ritz_gram)


def solution(mesh):
    placed = (
        P(None, "gx", "gy", None),
        P("gx", "gy", None),
        P(),
        P("gx", "gy", None),
        P("gx", "gy", None, None),
        P("gx", "gy"),
        P("gx", "gy", None, None),
    )
    return jax.shard_map(
        body,
        mesh=mesh,
        in_specs=placed,
        out_specs=(P(None, "gx", "gy", None), P(("gx", "gy"), None), P()),
        check_vma=False,
    )
```

profile of v0, /device:TPU:0, one launch (start us, length us, event | category | flops | bytes accessed | tf_op | source)
XLA Modules:
  0.0 530.0 jit_solution(1779432885856855623)
XLA Ops:
  0.7 10.1 %copy.60 = f32[16,16,32,256]{3,0,2,1:T(8,128)S(1)} copy(f32[16,16,32,256]{3,2,1,0:T(8,128)} %param.7) | data formatting | bytes 16777216 | tf_op args[0]
  10.8 2.4 collective-permute-start.1
  13.3 1.8 collective-permute-start
  16.0 10.0 %constant_dynamic-update-slice_fusion.1 = f32[16,18,32,256]{3,0,2,1:T(8,128)} fusion(f32[16,18,32,256]{3,0,2,1:T(8,128)} %constant_dynamic-update-slice_fusion.2, f32[16,16,32,256]{3,2,1,0:T(8,128)S(1)} %copy-done), kind=kLoop, calls=%fused_computation.202 | loop fusion | bytes 16777216
  28.0 1.3 collective-permute-start.2
  29.3 4.9 collective-permute-start.3
  34.9 2.1 multiply_add_fusion
  37.0 1.4 collective-permute-done.3
  38.4 25.3 %fusion.81 = f32[16,16,32,256]{3,0,2,1:T(8,128)} fusion(f32[16,16,32,256]{3,0,2,1:T(8,128)} %copy-done.2, f32[16,18,32,256]{3,0,2,1:T(8,128)} %constant_dynamic-update-slice_fusion, f32[16,18,1,256]{3,0,2,1:T(8,128)S(1)} %collective-permute-done.3, f32[16,18,1,256]{3,0,2,1:T(8,128)S(1)} %collective-permute-done.2, ...), kind=kLoop, calls=%fused_computation.158 | loop fusion | flops 41943040 | bytes 29032460 | tf_op jit(solution)/shard_map/jit(_where)/select_n | solution.py:42
  65.0 1.3 collective-permute-start.4
  66.3 7.8 %collective-permute-start.5 = (f32[16,1,32,256]{3,0,2,1:T(8,128)S(1)}, f32[16,1,32,256]{3,0,2,1:T(8,128)S(1)}, u32[]{:S(2)}, u32[]{:S(2)}) collective-permute-start(f32[16,1,32,256]{3,0,2,1:T(8,128)S(1)} %get-tuple-element.40), channel_id=1, source_target_pairs={{0,4},{4,8},{8,12},{12,16},{16,20},{20,24},{24,28},{1,5},{5,9},{9,... | collective-permute-start | bytes 1572872 | tf_op jit(solution)/shard_map/ppermute | solution.py:19
  74.1 1.5 collective-permute-done.5
  76.7 1.3 collective-permute-start.6
  78.0 4.9 collective-permute-start.7
  82.9 2.6 collective-permute-done.6
  85.5 1.5 collective-permute-done.7
  86.9 24.8 %fusion.87 = f32[16,16,32,256]{3,0,2,1:T(8,128)} fusion(f32[16,16,32,256]{3,0,2,1:T(8,128)} %fusion.81, f32[16,1,32,256]{3,0,2,1:T(8,128)S(1)} %collective-permute-done.4, f32[16,1,32,256]{3,0,2,1:T(8,128)S(1)} %collective-permute-done.5, f32[16,18,1,256]{3,0,2,1:T(8,128)S(1)} %collective-permute-done.7, f32[16,18,1,256]{3,0,2,1:T(8,128)S(1)} %collective-permute-done.6, ...), kind=kLoop, calls=%fused_computation.164 | loop fusion | flops 50331648 | bytes 27983884 | tf_op jit(solution)/shard_map/jit(_where)/select_n | solution.py:42
  113.1 1.3 collective-permute-start.8
  114.4 12.9 %collective-permute-start.9 = (f32[16,1,32,256]{3,0,2,1:T(8,128)S(1)}, f32[16,1,32,256]{3,0,2,1:T(8,128)S(1)}, u32[]{:S(2)}, u32[]{:S(2)}) collective-permute-start(f32[16,1,32,256]{3,0,2,1:T(8,128)S(1)} %get-tuple-element.38), channel_id=1, source_target_pairs={{0,4},{4,8},{8,12},{12,16},{16,20},{20,24},{24,28},{1,5},{5,9},{9,... | collective-permute-start | bytes 1572872 | tf_op jit(solution)/shard_map/ppermute | solution.py:19
  127.3 1.5 collective-permute-done.9
  129.9 1.3 collective-permute-start.10
  131.2 4.7 collective-permute-start.11
  135.9 2.7 collective-permute-done.10
  138.6 1.5 collective-permute-done.11
  140.1 24.8 %fusion.86 = f32[16,16,32,256]{3,0,2,1:T(8,128)} fusion(f32[16,16,32,256]{3,0,2,1:T(8,128)} %fusion.87, f32[16,1,32,256]{3,0,2,1:T(8,128)S(1)} %collective-permute-done.8, f32[16,1,32,256]{3,0,2,1:T(8,128)S(1)} %collective-permute-done.9, f32[16,18,1,256]{3,0,2,1:T(8,128)S(1)} %collective-permute-done.11, ...), kind=kLoop, calls=%fused_computation.163 | loop fusion | flops 50331648 | bytes 27983884 | tf_op jit(solution)/shard_map/jit(_where)/select_n | solution.py:42
  166.1 1.3 collective-permute-start.12
  167.4 10.1 %collective-permute-start.13 = (f32[16,1,32,256]{3,0,2,1:T(8,128)S(1)}, f32[16,1,32,256]{3,0,2,1:T(8,128)S(1)}, u32[]{:S(2)}, u32[]{:S(2)}) collective-permute-start(f32[16,1,32,256]{3,0,2,1:T(8,128)S(1)} %get-tuple-element.36), channel_id=1, source_target_pairs={{0,4},{4,8},{8,12},{12,16},{16,20},{20,24},{24,28},{1,5},{5,9},{9,... | collective-permute-start | bytes 1572872 | tf_op jit(solution)/shard_map/ppermute | solution.py:19
  177.6 1.5 collective-permute-done.13
  180.1 1.3 collective-permute-start.14
  181.4 4.8 collective-permute-start.15
  186.3 2.7 collective-permute-done.14
  189.0 1.5 collective-permute-done.15
  190.5 24.2 %fusion.85 = f32[16,16,32,256]{3,0,2,1:T(8,128)S(1)} fusion(f32[16,16,32,256]{3,0,2,1:T(8,128)} %fusion.86, f32[16,1,32,256]{3,0,2,1:T(8,128)S(1)} %collective-permute-done.12, f32[16,1,32,256]{3,0,2,1:T(8,128)S(1)} %collective-permute-done.13, f32[16,18,1,256]{3,0,2,1:T(8,128)S(1)} %collective-permute-done.15, ...), kind=kLoop, calls=%fused_computation.162 | loop fusion | flops 50331648 | bytes 27983884 | tf_op jit(solution)/shard_map/jit(_where)/select_n | solution.py:42
  214.8 1.3 collective-permute-start.16
  216.1 9.8 %collective-permute-start.17 = (f32[16,1,32,256]{3,0,2,1:T(8,128)S(1)}, f32[16,1,32,256]{3,0,2,1:T(8,128)S(1)}, u32[]{:S(2)}, u32[]{:S(2)}) collective-permute-start(f32[16,1,32,256]{3,0,2,1:T(8,128)S(1)} %get-tuple-element.34), channel_id=1, source_target_pairs={{0,4},{4,8},{8,12},{12,16},{16,20},{20,24},{24,28},{1,5},{5,9},{9,... | collective-permute-start | bytes 1572872 | tf_op jit(solution)/shard_map/ppermute | solution.py:19
  225.9 1.5 collective-permute-done.17
  228.7 5.1 collective-permute-start.19
  233.8 2.5 collective-permute-done.18
  236.3 1.5 collective-permute-done.19
  237.8 13.1 %fusion.80 = f32[16,16,32,256]{3,0,2,1:T(8,128)} fusion(f32[16,16,32,256]{3,0,2,1:T(8,128)S(1)} %fusion.85, f32[16,1,32,256]{3,0,2,1:T(8,128)S(1)} %collective-permute-done.16, f32[16,1,32,256]{3,0,2,1:T(8,128)S(1)} %collective-permute-done.17, f32[16,18,1,256]{3,0,2,1:T(8,128)S(1)} %collective-permute-done.19, ...), kind=kLoop, calls=%fused_computation.157 | loop fusion | flops 50331648 | bytes 19595276 | tf_op jit(solution)/shard_map/jit(_where)/select_n | solution.py:42
  253.5 9.8 %collective-permute-start.21 = (f32[16,1,32,256]{3,0,2,1:T(8,128)S(1)}, f32[16,1,32,256]{3,0,2,1:T(8,128)S(1)}, u32[]{:S(2)}, u32[]{:S(2)}) collective-permute-start(f32[16,1,32,256]{3,0,2,1:T(8,128)S(1)} %get-tuple-element.32), channel_id=1, source_target_pairs={{0,4},{4,8},{8,12},{12,16},{16,20},{20,24},{24,28},{1,5},{5,9},{9,... | collective-permute-start | bytes 1572872 | tf_op jit(solution)/shard_map/ppermute | solution.py:19
  263.3 1.5 collective-permute-done.21
  267.1 4.8 collective-permute-start.23
  272.0 2.7 collective-permute-done.22
  274.7 1.5 collective-permute-done.23
  276.2 22.7 %fusion.84 = f32[16,16,32,256]{3,0,2,1:T(8,128)} fusion(f32[16,16,32,256]{3,0,2,1:T(8,128)S(1)} %fusion.85, f32[16,16,32,256]{3,0,2,1:T(8,128)} %fusion.80, f32[16,1,32,256]{3,0,2,1:T(8,128)S(1)} %collective-permute-done.20, f32[16,1,32,256]{3,0,2,1:T(8,128)S(1)} %collective-permute-done.21, f32[16,18,1,256]{3,0,2,1:T(8,128)S(1)} %collective-permute-done.23, ...), kind=kLoop, calls=%fused_computation.161 | loop fusion | flops 50331648 | bytes 27983884 | tf_op jit(solution)/shard_map/jit(_where)/select_n | solution.py:42
  300.2 1.3 collective-permute-start.24
  301.5 11.3 %collective-permute-start.25 = (f32[16,1,32,256]{3,0,2,1:T(8,128)S(1)}, f32[16,1,32,256]{3,0,2,1:T(8,128)S(1)}, u32[]{:S(2)}, u32[]{:S(2)}) collective-permute-start(f32[16,1,32,256]{3,0,2,1:T(8,128)S(1)} %get-tuple-element.30), channel_id=1, source_target_pairs={{0,4},{4,8},{8,12},{12,16},{16,20},{20,24},{24,28},{1,5},{5,9},{9,... | collective-permute-start | bytes 1572872 | tf_op jit(solution)/shard_map/ppermute | solution.py:19
  312.8 1.5 collective-permute-done.25
  316.7 4.7 collective-permute-start.27
  322.1 2.1 collective-permute-done.26
  324.2 1.5 collective-permute-done.27
  325.6 22.7 %fusion.83 = f32[16,16,32,256]{3,0,2,1:T(8,128)} fusion(f32[16,16,32,256]{3,0,2,1:T(8,128)S(1)} %fusion.85, f32[16,16,32,256]{3,0,2,1:T(8,128)} %fusion.84, f32[16,1,32,256]{3,0,2,1:T(8,128)S(1)} %collective-permute-done.24, f32[16,1,32,256]{3,0,2,1:T(8,128)S(1)} %collective-permute-done.25, f32[16,18,1,256]{3,0,2,1:T(8,128)S(1)} %collective-permute-done.27, ...), kind=kLoop, calls=%fused_computation.160 | loop fusion | flops 50331648 | bytes 27983884 | tf_op jit(solution)/shard_map/jit(_where)/select_n | solution.py:42
  350.9 13.9 %collective-permute-start.29 = (f32[16,1,32,256]{3,0,2,1:T(8,128)S(1)}, f32[16,1,32,256]{3,0,2,1:T(8,128)S(1)}, u32[]{:S(2)}, u32[]{:S(2)}) collective-permute-start(f32[16,1,32,256]{3,0,2,1:T(8,128)S(1)} %get-tuple-element.28), channel_id=1, source_target_pairs={{0,4},{4,8},{8,12},{12,16},{16,20},{20,24},{24,28},{1,5},{5,9},{9,... | collective-permute-start | bytes 1572872 | tf_op jit(solution)/shard_map/ppermute | solution.py:19
  367.4 1.3 collective-permute-start.30
  368.7 4.7 collective-permute-start.31
  373.5 2.7 collective-permute-done.30
  376.2 1.5 collective-permute-done.31
  377.7 22.7 %fusion.82 = f32[16,16,32,256]{3,0,2,1:T(8,128)} fusion(f32[16,16,32,256]{3,0,2,1:T(8,128)S(1)} %fusion.85, f32[16,16,32,256]{3,0,2,1:T(8,128)} %fusion.83, f32[16,1,32,256]{3,0,2,1:T(8,128)S(1)} %collective-permute-done.28, f32[16,1,32,256]{3,0,2,1:T(8,128)S(1)} %collective-permute-done.29, f32[16,18,1,256]{3,0,2,1:T(8,128)S(1)} %collective-permute-done.31, ...), kind=kLoop, calls=%fused_computation.159 | loop fusion | flops 50331648 | bytes 27983884 | tf_op jit(solution)/shard_map/jit(_where)/select_n | solution.py:42
  400.4 32.9 %copy.61 = f32[16,16,32,256]{0,3,2,1:T(8,128)} copy(f32[16,16,32,256]{3,0,2,1:T(8,128)} %fusion.82) | data formatting | bytes 16777216 | tf_op jit(solution)/shard_map/jit(_where)/select_n | solution.py:42
  433.3 1.8 gather_fusion
  436.0 39.7 %all-to-all-start = ((f32[32,1,128]{2,1,0:T(1,128)}), f32[32,1,128]{2,1,0:T(1,128)S(1)}, u32[]{:S(2)}, u32[]{:S(2)}) async-start(f32[32,1,128]{2,1,0:T(1,128)} %reshape.93), calls=%async_computation | async-start | bytes 32768 | tf_op jit(solution)/shard_map/all_to_all | solution.py:74
  475.7 11.6 %copy.66 = f32[16,16,32,256]{3,2,1,0:T(8,128)} copy(f32[16,16,32,256]{3,0,2,1:T(8,128)} %fusion.82) | data formatting | bytes 16777216
  489.2 40.6 %psum.7 = f32[16,16]{1,0:T(8,128)} all-reduce(f32[16,16]{1,0:T(8,128)S(1)} %fusion.109), channel_id=1, replica_groups=mesh['gx'=8,'gy'=4] {'gx','gy'}, use_global_device_ids=true, to_apply=%region_1.2 | all-reduce | flops 256 | bytes 2048 | tf_op jit(solution)/shard_map/psum | solution.py:81
  (68 shorter events, 28.4 us)
Async XLA Ops:
  0.6 15.4 %copy-start = (f32[16,16,32,256]{3,2,1,0:T(8,128)S(1)}, f32[16,16,32,256]{3,2,1,0:T(8,128)}, u32[]{:S(2)}) copy-start(f32[16,16,32,256]{3,2,1,0:T(8,128)} %param.7) | copy-start | bytes 25165828
  0.6 14.4 %copy-start.1 = (f32[16,32,256]{2,1,0:T(8,128)S(1)}, f32[16,32,256]{2,1,0:T(8,128)}, u32[]{:S(2)}) copy-start(f32[16,32,256]{2,1,0:T(8,128)} %param.8) | copy-start | bytes 1572868
  10.7 15.3 %copy-start.2 = (f32[16,16,32,256]{3,0,2,1:T(8,128)}, f32[16,16,32,256]{3,0,2,1:T(8,128)S(1)}, u32[]{:S(2)}) copy-start(f32[16,16,32,256]{3,0,2,1:T(8,128)S(1)} %copy.60) | copy-start | bytes 25165828
  10.8 4.4 collective-permute-start.1
  13.3 12.8 %collective-permute-start = (f32[16,1,32,256]{3,0,2,1:T(8,128)S(1)}, f32[16,1,32,256]{3,0,2,1:T(8,128)S(1)}, u32[]{:S(2)}, u32[]{:S(2)}) collective-permute-start(f32[16,1,32,256]{3,0,2,1:T(8,128)S(1)} %get-tuple-element.42), channel_id=1, source_target_pairs={{4,0},{8,4},{12,8},{16,12},{20,16},{24,20},{28,24},{5,1},{9,5},{13... | collective-permute-start | bytes 1572872 | tf_op jit(solution)/shard_map/ppermute | solution.py:21
  16.0 18.2 %copy-start.5 = (f32[3]{0:T(128)S(1)}, f32[3]{0:T(128)}, u32[]{:S(2)}) copy-start(f32[3]{0:T(128)} %param.9) | copy-start | bytes 40
  28.0 9.0 %collective-permute-start.2 = (f32[16,18,1,256]{3,0,2,1:T(8,128)S(1)}, f32[16,18,1,256]{3,0,2,1:T(8,128)S(1)}, u32[]{:S(2)}, u32[]{:S(2)}) collective-permute-start(f32[16,18,1,256]{3,0,2,1:T(8,128)S(1)} %get-tuple-element.26), channel_id=1, source_target_pairs={{1,0},{2,1},{3,2},{5,4},{6,5},{7,6},{9,8},{10,9},{11,10},{13,12},{... | collective-permute-start | bytes 884744 | tf_op jit(solution)/shard_map/ppermute | solution.py:21
  29.3 9.2 %collective-permute-start.3 = (f32[16,18,1,256]{3,0,2,1:T(8,128)S(1)}, f32[16,18,1,256]{3,0,2,1:T(8,128)S(1)}, u32[]{:S(2)}, u32[]{:S(2)}) collective-permute-start(f32[16,18,1,256]{3,0,2,1:T(8,128)S(1)} %get-tuple-element.27), channel_id=1, source_target_pairs={{0,1},{1,2},{2,3},{4,5},{5,6},{6,7},{8,9},{9,10},{10,11},{12,13},{... | collective-permute-start | bytes 884744 | tf_op jit(solution)/shard_map/ppermute | solution.py:19
  65.0 9.1 %collective-permute-start.4 = (f32[16,1,32,256]{3,0,2,1:T(8,128)S(1)}, f32[16,1,32,256]{3,0,2,1:T(8,128)S(1)}, u32[]{:S(2)}, u32[]{:S(2)}) collective-permute-start(f32[16,1,32,256]{3,0,2,1:T(8,128)S(1)} %get-tuple-element.41), channel_id=1, source_target_pairs={{4,0},{8,4},{12,8},{16,12},{20,16},{24,20},{28,24},{5,1},{9,5},{13... | collective-permute-start | bytes 1572872 | tf_op jit(solution)/shard_map/ppermute | solution.py:21
  66.3 9.3 %collective-permute-start.5 = (f32[16,1,32,256]{3,0,2,1:T(8,128)S(1)}, f32[16,1,32,256]{3,0,2,1:T(8,128)S(1)}, u32[]{:S(2)}, u32[]{:S(2)}) collective-permute-start(f32[16,1,32,256]{3,0,2,1:T(8,128)S(1)} %get-tuple-element.40), channel_id=1, source_target_pairs={{0,4},{4,8},{8,12},{12,16},{16,20},{20,24},{24,28},{1,5},{5,9},{9,... | collective-permute-start | bytes 1572872 | tf_op jit(solution)/shard_map/ppermute | solution.py:19
  76.7 8.8 %collective-permute-start.6 = (f32[16,18,1,256]{3,0,2,1:T(8,128)S(1)}, f32[16,18,1,256]{3,0,2,1:T(8,128)S(1)}, u32[]{:S(2)}, u32[]{:S(2)}) collective-permute-start(f32[16,18,1,256]{3,0,2,1:T(8,128)S(1)} %get-tuple-element.24), channel_id=1, source_target_pairs={{1,0},{2,1},{3,2},{5,4},{6,5},{7,6},{9,8},{10,9},{11,10},{13,12},{... | collective-permute-start | bytes 884744 | tf_op jit(solution)/shard_map/ppermute | solution.py:21
  78.0 8.9 %collective-permute-start.7 = (f32[16,18,1,256]{3,0,2,1:T(8,128)S(1)}, f32[16,18,1,256]{3,0,2,1:T(8,128)S(1)}, u32[]{:S(2)}, u32[]{:S(2)}) collective-permute-start(f32[16,18,1,256]{3,0,2,1:T(8,128)S(1)} %get-tuple-element.25), channel_id=1, source_target_pairs={{0,1},{1,2},{2,3},{4,5},{5,6},{6,7},{8,9},{9,10},{10,11},{12,13},{... | collective-permute-start | bytes 884744 | tf_op jit(solution)/shard_map/ppermute | solution.py:19
  113.1 14.2 %collective-permute-start.8 = (f32[16,1,32,256]{3,0,2,1:T(8,128)S(1)}, f32[16,1,32,256]{3,0,2,1:T(8,128)S(1)}, u32[]{:S(2)}, u32[]{:S(2)}) collective-permute-start(f32[16,1,32,256]{3,0,2,1:T(8,128)S(1)} %get-tuple-element.39), channel_id=1, source_target_pairs={{4,0},{8,4},{12,8},{16,12},{20,16},{24,20},{28,24},{5,1},{9,5},{13... | collective-permute-start | bytes 1572872 | tf_op jit(solution)/shard_map/ppermute | solution.py:21
  114.4 14.4 %collective-permute-start.9 = (f32[16,1,32,256]{3,0,2,1:T(8,128)S(1)}, f32[16,1,32,256]{3,0,2,1:T(8,128)S(1)}, u32[]{:S(2)}, u32[]{:S(2)}) collective-permute-start(f32[16,1,32,256]{3,0,2,1:T(8,128)S(1)} %get-tuple-element.38), channel_id=1, source_target_pairs={{0,4},{4,8},{8,12},{12,16},{16,20},{20,24},{24,28},{1,5},{5,9},{9,... | collective-permute-start | bytes 1572872 | tf_op jit(solution)/shard_map/ppermute | solution.py:19
  129.9 8.8 %collective-permute-start.10 = (f32[16,18,1,256]{3,0,2,1:T(8,128)S(1)}, f32[16,18,1,256]{3,0,2,1:T(8,128)S(1)}, u32[]{:S(2)}, u32[]{:S(2)}) collective-permute-start(f32[16,18,1,256]{3,0,2,1:T(8,128)S(1)} %get-tuple-element.22), channel_id=1, source_target_pairs={{1,0},{2,1},{3,2},{5,4},{6,5},{7,6},{9,8},{10,9},{11,10},{13,12},{... | collective-permute-start | bytes 884744 | tf_op jit(solution)/shard_map/ppermute | solution.py:21
  131.2 8.9 %collective-permute-start.11 = (f32[16,18,1,256]{3,0,2,1:T(8,128)S(1)}, f32[16,18,1,256]{3,0,2,1:T(8,128)S(1)}, u32[]{:S(2)}, u32[]{:S(2)}) collective-permute-start(f32[16,18,1,256]{3,0,2,1:T(8,128)S(1)} %get-tuple-element.23), channel_id=1, source_target_pairs={{0,1},{1,2},{2,3},{4,5},{5,6},{6,7},{8,9},{9,10},{10,11},{12,13},{... | collective-permute-start | bytes 884744 | tf_op jit(solution)/shard_map/ppermute | solution.py:19
  166.1 11.4 %collective-permute-start.12 = (f32[16,1,32,256]{3,0,2,1:T(8,128)S(1)}, f32[16,1,32,256]{3,0,2,1:T(8,128)S(1)}, u32[]{:S(2)}, u32[]{:S(2)}) collective-permute-start(f32[16,1,32,256]{3,0,2,1:T(8,128)S(1)} %get-tuple-element.37), channel_id=1, source_target_pairs={{4,0},{8,4},{12,8},{16,12},{20,16},{24,20},{28,24},{5,1},{9,5},{13... | collective-permute-start | bytes 1572872 | tf_op jit(solution)/shard_map/ppermute | solution.py:21
  167.4 11.6 %collective-permute-start.13 = (f32[16,1,32,256]{3,0,2,1:T(8,128)S(1)}, f32[16,1,32,256]{3,0,2,1:T(8,128)S(1)}, u32[]{:S(2)}, u32[]{:S(2)}) collective-permute-start(f32[16,1,32,256]{3,0,2,1:T(8,128)S(1)} %get-tuple-element.36), channel_id=1, source_target_pairs={{0,4},{4,8},{8,12},{12,16},{16,20},{20,24},{24,28},{1,5},{5,9},{9,... | collective-permute-start | bytes 1572872 | tf_op jit(solution)/shard_map/ppermute | solution.py:19
  180.1 8.9 %collective-permute-start.14 = (f32[16,18,1,256]{3,0,2,1:T(8,128)S(1)}, f32[16,18,1,256]{3,0,2,1:T(8,128)S(1)}, u32[]{:S(2)}, u32[]{:S(2)}) collective-permute-start(f32[16,18,1,256]{3,0,2,1:T(8,128)S(1)} %get-tuple-element.20), channel_id=1, source_target_pairs={{1,0},{2,1},{3,2},{5,4},{6,5},{7,6},{9,8},{10,9},{11,10},{13,12},{... | collective-permute-start | bytes 884744 | tf_op jit(solution)/shard_map/ppermute | solution.py:21
  181.4 9.1 %collective-permute-start.15 = (f32[16,18,1,256]{3,0,2,1:T(8,128)S(1)}, f32[16,18,1,256]{3,0,2,1:T(8,128)S(1)}, u32[]{:S(2)}, u32[]{:S(2)}) collective-permute-start(f32[16,18,1,256]{3,0,2,1:T(8,128)S(1)} %get-tuple-element.21), channel_id=1, source_target_pairs={{0,1},{1,2},{2,3},{4,5},{5,6},{6,7},{8,9},{9,10},{10,11},{12,13},{... | collective-permute-start | bytes 884744 | tf_op jit(solution)/shard_map/ppermute | solution.py:19
  214.8 11.1 %collective-permute-start.16 = (f32[16,1,32,256]{3,0,2,1:T(8,128)S(1)}, f32[16,1,32,256]{3,0,2,1:T(8,128)S(1)}, u32[]{:S(2)}, u32[]{:S(2)}) collective-permute-start(f32[16,1,32,256]{3,0,2,1:T(8,128)S(1)} %get-tuple-element.35), channel_id=1, source_target_pairs={{4,0},{8,4},{12,8},{16,12},{20,16},{24,20},{28,24},{5,1},{9,5},{13... | collective-permute-start | bytes 1572872 | tf_op jit(solution)/shard_map/ppermute | solution.py:21
  216.1 11.3 %collective-permute-start.17 = (f32[16,1,32,256]{3,0,2,1:T(8,128)S(1)}, f32[16,1,32,256]{3,0,2,1:T(8,128)S(1)}, u32[]{:S(2)}, u32[]{:S(2)}) collective-permute-start(f32[16,1,32,256]{3,0,2,1:T(8,128)S(1)} %get-tuple-element.34), channel_id=1, source_target_pairs={{0,4},{4,8},{8,12},{12,16},{16,20},{20,24},{24,28},{1,5},{5,9},{9,... | collective-permute-start | bytes 1572872 | tf_op jit(solution)/shard_map/ppermute | solution.py:19
  227.4 8.9 %collective-permute-start.18 = (f32[16,18,1,256]{3,0,2,1:T(8,128)S(1)}, f32[16,18,1,256]{3,0,2,1:T(8,128)S(1)}, u32[]{:S(2)}, u32[]{:S(2)}) collective-permute-start(f32[16,18,1,256]{3,0,2,1:T(8,128)S(1)} %get-tuple-element.18), channel_id=1, source_target_pairs={{1,0},{2,1},{3,2},{5,4},{6,5},{7,6},{9,8},{10,9},{11,10},{13,12},{... | collective-permute-start | bytes 884744 | tf_op jit(solution)/shard_map/ppermute | solution.py:21
  228.7 9.1 %collective-permute-start.19 = (f32[16,18,1,256]{3,0,2,1:T(8,128)S(1)}, f32[16,18,1,256]{3,0,2,1:T(8,128)S(1)}, u32[]{:S(2)}, u32[]{:S(2)}) collective-permute-start(f32[16,18,1,256]{3,0,2,1:T(8,128)S(1)} %get-tuple-element.19), channel_id=1, source_target_pairs={{0,1},{1,2},{2,3},{4,5},{5,6},{6,7},{8,9},{9,10},{10,11},{12,13},{... | collective-permute-start | bytes 884744 | tf_op jit(solution)/shard_map/ppermute | solution.py:19
  252.2 11.1 %collective-permute-start.20 = (f32[16,1,32,256]{3,0,2,1:T(8,128)S(1)}, f32[16,1,32,256]{3,0,2,1:T(8,128)S(1)}, u32[]{:S(2)}, u32[]{:S(2)}) collective-permute-start(f32[16,1,32,256]{3,0,2,1:T(8,128)S(1)} %get-tuple-element.33), channel_id=1, source_target_pairs={{4,0},{8,4},{12,8},{16,12},{20,16},{24,20},{28,24},{5,1},{9,5},{13... | collective-permute-start | bytes 1572872 | tf_op jit(solution)/shard_map/ppermute | solution.py:21
  253.5 11.3 %collective-permute-start.21 = (f32[16,1,32,256]{3,0,2,1:T(8,128)S(1)}, f32[16,1,32,256]{3,0,2,1:T(8,128)S(1)}, u32[]{:S(2)}, u32[]{:S(2)}) collective-permute-start(f32[16,1,32,256]{3,0,2,1:T(8,128)S(1)} %get-tuple-element.32), channel_id=1, source_target_pairs={{0,4},{4,8},{8,12},{12,16},{16,20},{20,24},{24,28},{1,5},{5,9},{9,... | collective-permute-start | bytes 1572872 | tf_op jit(solution)/shard_map/ppermute | solution.py:19
  265.8 8.9 %collective-permute-start.22 = (f32[16,18,1,256]{3,0,2,1:T(8,128)S(1)}, f32[16,18,1,256]{3,0,2,1:T(8,128)S(1)}, u32[]{:S(2)}, u32[]{:S(2)}) collective-permute-start(f32[16,18,1,256]{3,0,2,1:T(8,128)S(1)} %get-tuple-element.16), channel_id=1, source_target_pairs={{1,0},{2,1},{3,2},{5,4},{6,5},{7,6},{9,8},{10,9},{11,10},{13,12},{... | collective-permute-start | bytes 884744 | tf_op jit(solution)/shard_map/ppermute | solution.py:21
  267.1 9.1 %collective-permute-start.23 = (f32[16,18,1,256]{3,0,2,1:T(8,128)S(1)}, f32[16,18,1,256]{3,0,2,1:T(8,128)S(1)}, u32[]{:S(2)}, u32[]{:S(2)}) collective-permute-start(f32[16,18,1,256]{3,0,2,1:T(8,128)S(1)} %get-tuple-element.17), channel_id=1, source_target_pairs={{0,1},{1,2},{2,3},{4,5},{5,6},{6,7},{8,9},{9,10},{10,11},{12,13},{... | collective-permute-start | bytes 884744 | tf_op jit(solution)/shard_map/ppermute | solution.py:19
  300.2 12.6 %collective-permute-start.24 = (f32[16,1,32,256]{3,0,2,1:T(8,128)S(1)}, f32[16,1,32,256]{3,0,2,1:T(8,128)S(1)}, u32[]{:S(2)}, u32[]{:S(2)}) collective-permute-start(f32[16,1,32,256]{3,0,2,1:T(8,128)S(1)} %get-tuple-element.31), channel_id=1, source_target_pairs={{4,0},{8,4},{12,8},{16,12},{20,16},{24,20},{28,24},{5,1},{9,5},{13... | collective-permute-start | bytes 1572872 | tf_op jit(solution)/shard_map/ppermute | solution.py:21
  301.5 12.8 %collective-permute-start.25 = (f32[16,1,32,256]{3,0,2,1:T(8,128)S(1)}, f32[16,1,32,256]{3,0,2,1:T(8,128)S(1)}, u32[]{:S(2)}, u32[]{:S(2)}) collective-permute-start(f32[16,1,32,256]{3,0,2,1:T(8,128)S(1)} %get-tuple-element.30), channel_id=1, source_target_pairs={{0,4},{4,8},{8,12},{12,16},{16,20},{20,24},{24,28},{1,5},{5,9},{9,... | collective-permute-start | bytes 1572872 | tf_op jit(solution)/shard_map/ppermute | solution.py:19
  315.4 8.8 %collective-permute-start.26 = (f32[16,18,1,256]{3,0,2,1:T(8,128)S(1)}, f32[16,18,1,256]{3,0,2,1:T(8,128)S(1)}, u32[]{:S(2)}, u32[]{:S(2)}) collective-permute-start(f32[16,18,1,256]{3,0,2,1:T(8,128)S(1)} %get-tuple-element.14), channel_id=1, source_target_pairs={{1,0},{2,1},{3,2},{5,4},{6,5},{7,6},{9,8},{10,9},{11,10},{13,12},{... | collective-permute-start | bytes 884744 | tf_op jit(solution)/shard_map/ppermute | solution.py:21
  316.7 8.9 %collective-permute-start.27 = (f32[16,18,1,256]{3,0,2,1:T(8,128)S(1)}, f32[16,18,1,256]{3,0,2,1:T(8,128)S(1)}, u32[]{:S(2)}, u32[]{:S(2)}) collective-permute-start(f32[16,18,1,256]{3,0,2,1:T(8,128)S(1)} %get-tuple-element.15), channel_id=1, source_target_pairs={{0,1},{1,2},{2,3},{4,5},{5,6},{6,7},{8,9},{9,10},{10,11},{12,13},{... | collective-permute-start | bytes 884744 | tf_op jit(solution)/shard_map/ppermute | solution.py:19
  322.1 42.8 %copy-start.7 = (s32[1,1,128,1]{2,3,1,0:T(1,128)S(1)}, s32[1,1,128,1]{2,3,1,0:T(1,128)}, u32[]{:S(2)}) copy-start(s32[1,1,128,1]{2,3,1,0:T(1,128)} %param.11) | copy-start | bytes 1540
  322.1 43.0 %copy-start.6 = (s32[1,1,128]{2,1,0:T(1,128)S(1)}, s32[1,1,128]{2,1,0:T(1,128)}, u32[]{:S(2)}) copy-start(s32[1,1,128]{2,1,0:T(1,128)} %param.10) | copy-start | bytes 1540
  349.6 15.5 %collective-permute-start.28 = (f32[16,1,32,256]{3,0,2,1:T(8,128)S(1)}, f32[16,1,32,256]{3,0,2,1:T(8,128)S(1)}, u32[]{:S(2)}, u32[]{:S(2)}) collective-permute-start(f32[16,1,32,256]{3,0,2,1:T(8,128)S(1)} %get-tuple-element.29), channel_id=1, source_target_pairs={{4,0},{8,4},{12,8},{16,12},{20,16},{24,20},{28,24},{5,1},{9,5},{13... | collective-permute-start | bytes 1572872 | tf_op jit(solution)/shard_map/ppermute | solution.py:21
  350.9 15.4 %collective-permute-start.29 = (f32[16,1,32,256]{3,0,2,1:T(8,128)S(1)}, f32[16,1,32,256]{3,0,2,1:T(8,128)S(1)}, u32[]{:S(2)}, u32[]{:S(2)}) collective-permute-start(f32[16,1,32,256]{3,0,2,1:T(8,128)S(1)} %get-tuple-element.28), channel_id=1, source_target_pairs={{0,4},{4,8},{8,12},{12,16},{16,20},{20,24},{24,28},{1,5},{5,9},{9,... | collective-permute-start | bytes 1572872 | tf_op jit(solution)/shard_map/ppermute | solution.py:19
  367.4 8.8 %collective-permute-start.30 = (f32[16,18,1,256]{3,0,2,1:T(8,128)S(1)}, f32[16,18,1,256]{3,0,2,1:T(8,128)S(1)}, u32[]{:S(2)}, u32[]{:S(2)}) collective-permute-start(f32[16,18,1,256]{3,0,2,1:T(8,128)S(1)} %get-tuple-element.12), channel_id=1, source_target_pairs={{1,0},{2,1},{3,2},{5,4},{6,5},{7,6},{9,8},{10,9},{11,10},{13,12},{... | collective-permute-start | bytes 884744 | tf_op jit(solution)/shard_map/ppermute | solution.py:21
  368.7 8.9 %collective-permute-start.31 = (f32[16,18,1,256]{3,0,2,1:T(8,128)S(1)}, f32[16,18,1,256]{3,0,2,1:T(8,128)S(1)}, u32[]{:S(2)}, u32[]{:S(2)}) collective-permute-start(f32[16,18,1,256]{3,0,2,1:T(8,128)S(1)} %get-tuple-element.13), channel_id=1, source_target_pairs={{0,1},{1,2},{2,3},{4,5},{5,6},{6,7},{8,9},{9,10},{10,11},{12,13},{... | collective-permute-start | bytes 884744 | tf_op jit(solution)/shard_map/ppermute | solution.py:19
  400.4 34.7 %copy-start.4 = (f32[1,1,128,16]{2,3,1,0:T(8,128)S(1)}, f32[1,1,128,16]{2,3,1,0:T(8,128)}, u32[]{:S(2)}) copy-start(f32[1,1,128,16]{2,3,1,0:T(8,128)} %param.13) | copy-start | bytes 24580
  436.0 51.3 %all-to-all-start = ((f32[32,1,128]{2,1,0:T(1,128)}), f32[32,1,128]{2,1,0:T(1,128)S(1)}, u32[]{:S(2)}, u32[]{:S(2)}) async-start(f32[32,1,128]{2,1,0:T(1,128)} %reshape.93), calls=%async_computation | async-start | bytes 32768 | tf_op jit(solution)/shard_map/all_to_all | solution.py:74
  488.9 40.8 %copy-start.3 = (f32[16,16]{1,0:T(8,128)}, f32[16,16]{1,0:T(8,128)S(1)}, u32[]{:S(2)}) copy-start(f32[16,16]{1,0:T(8,128)S(1)} %convolution_bitcast_fusion) | copy-start | bytes 3076
where the time goes:
time: 538 us; the launch traced here: 530 us
  other arithmetic  190 us (35%)
  starting transfers between devices  178 us (33%)
  local copies, waits for them, and re-layouts  79 us (15%)
  blocking collectives  40.6 us (8%)
  waiting for transfers between devices  39.9 us (7%)
    select_n x8, other arithmetic, relax(): return jnp.where(diffusion > 0.0, updated, 0.0)  180 us
    ppermute x16, starting transfers between devices, padded_2(): lax.ppermute(tail, axis, [(i, (i + 1) % count) for i in range(ends)])  117 us
    psum x1, blocking collectives, body(): lax.psum(jnp.dot(goal_block.T, goal_block, precision=lax.Precision.HIGHES...  40.6 us
    all_to_all x1, starting transfers between devices, body(): lax.all_to_all(outgoing, ('gx', 'gy'), split_axis=0, concat_axis=0, tiled...  39.7 us
    unnamed x22, local copies, waits for them, and re-layouts  33.4 us
    select_n x1, local copies, waits for them, and re-layouts, relax(): return jnp.where(diffusion > 0.0, updated, 0.0)  32.9 us
    ppermute x16, waiting for transfers between devices, padded_2(): lax.ppermute(tail, axis, [(i, (i + 1) % count) for i in range(ends)])  21.8 us
    ppermute x16, starting transfers between devices, padded_2(): lax.ppermute(head, axis, [((i + 1) % count, i) for i in range(ends)])  21.2 us
  transfers between devices with their start and end apart: 33, of which 22 were waited for; matrix products, arithmetic and copies ran while one was open for 5% of the time, Pallas kernels for 0%

commit v1 on v0

--- a/solution.py
+++ b/solution.py
@@ -79,7 +79,7 @@
         precision=lax.Precision.HIGHEST,
     )
     ritz_gram = lax.psum(
-        jnp.dot(goal_block.T, goal_block, precision=lax.Precision.HIGHEST), ("gx", "gy")
+        lax.psum(jnp.dot(goal_block.T, goal_block, precision=lax.Precision.HIGHEST), "gy"), "gx"
     )
     return (state_field, goal_block, ritz_gram)
 

time: 538 us -> 522 us (0.970)
  blocking collectives: 40.6 us -> 25 us
    psum x1, blocking collectives: 40.6 us -> 12.2 us  [body(): lax.psum(jnp.dot(goal_block.T, goal_block, precision=lax.Precision.HIGHES...]
    psum x0 -> x1, blocking collectives: none -> 12.7 us  [body(): lax.psum(lax.psum(jnp.dot(goal_block.T, goal_block, precision=lax.Precisi...]
  transfers between devices with their start and end apart: 33 -> 33, of which waited for: 22 -> 23; matrix products, arithmetic and copies ran while one was open for 5% -> 5% of each run, Pallas kernels for 0% -> 0%
where the time goes in v1:
time: 522 us; the launch traced here: 514 us
  other arithmetic  189 us (36%)
  starting transfers between devices  178 us (34%)
  local copies, waits for them, and re-layouts  79 us (15%)
  waiting for transfers between devices  40 us (8%)
  blocking collectives  25 us (5%)
    select_n x8, other arithmetic, relax(): return jnp.where(diffusion > 0.0, updated, 0.0)  180 us
    ppermute x16, starting transfers between devices, padded_2(): lax.ppermute(tail, axis, [(i, (i + 1) % count) for i in range(ends)])  117 us
    all_to_all x1, starting transfers between devices, body(): lax.all_to_all(outgoing, ('gx', 'gy'), split_axis=0, concat_axis=0, tiled...  39.7 us
    unnamed x22, local copies, waits for them, and re-layouts  33.4 us
    select_n x1, local copies, waits for them, and re-layouts, relax(): return jnp.where(diffusion > 0.0, updated, 0.0)  32.9 us
    ppermute x16, waiting for transfers between devices, padded_2(): lax.ppermute(tail, axis, [(i, (i + 1) % count) for i in range(ends)])  21.8 us
    ppermute x16, starting transfers between devices, padded_2(): lax.ppermute(head, axis, [((i + 1) % count, i) for i in range(ends)])  21.2 us
    ppermute x16, waiting for transfers between devices, padded_2(): lax.ppermute(head, axis, [((i + 1) % count, i) for i in range(ends)])  18.2 us
  transfers between devices with their start and end apart: 33, of which 23 were waited for; matrix products, arithmetic and copies ran while one was open for 5% of the time, Pallas kernels for 0%

profile of v1, /device:TPU:0, one launch (start us, length us, event | category | flops | bytes accessed | tf_op | source)
XLA Modules:
  0.0 513.9 jit_solution(16442050574768679717)
XLA Ops:
  0.7 10.1 %copy.60 = f32[16,16,32,256]{3,0,2,1:T(8,128)S(1)} copy(f32[16,16,32,256]{3,2,1,0:T(8,128)} %param.7) | data formatting | bytes 16777216 | tf_op args[0]
  10.8 2.4 collective-permute-start.1
  13.3 1.8 collective-permute-start
  16.0 10.0 %constant_dynamic-update-slice_fusion.1 = f32[16,18,32,256]{3,0,2,1:T(8,128)} fusion(f32[16,18,32,256]{3,0,2,1:T(8,128)} %constant_dynamic-update-slice_fusion.2, f32[16,16,32,256]{3,2,1,0:T(8,128)S(1)} %copy-done), kind=kLoop, calls=%fused_computation.202 | loop fusion | bytes 16777216
  28.0 1.3 collective-permute-start.2
  29.3 4.9 collective-permute-start.3
  34.8 2.0 multiply_add_fusion
  37.0 1.5 collective-permute-done.3
  38.4 25.3 %fusion.81 = f32[16,16,32,256]{3,0,2,1:T(8,128)} fusion(f32[16,16,32,256]{3,0,2,1:T(8,128)} %copy-done.2, f32[16,18,32,256]{3,0,2,1:T(8,128)} %constant_dynamic-update-slice_fusion, f32[16,18,1,256]{3,0,2,1:T(8,128)S(1)} %collective-permute-done.3, f32[16,18,1,256]{3,0,2,1:T(8,128)S(1)} %collective-permute-done.2, ...), kind=kLoop, calls=%fused_computation.158 | loop fusion | flops 41943040 | bytes 29032460 | tf_op jit(solution)/shard_map/jit(_where)/select_n | solution.py:42
  65.0 1.3 collective-permute-start.4
  66.3 7.8 %collective-permute-start.5 = (f32[16,1,32,256]{3,0,2,1:T(8,128)S(1)}, f32[16,1,32,256]{3,0,2,1:T(8,128)S(1)}, u32[]{:S(2)}, u32[]{:S(2)}) collective-permute-start(f32[16,1,32,256]{3,0,2,1:T(8,128)S(1)} %get-tuple-element.40), channel_id=1, source_target_pairs={{0,4},{4,8},{8,12},{12,16},{16,20},{20,24},{24,28},{1,5},{5,9},{9,... | collective-permute-start | bytes 1572872 | tf_op jit(solution)/shard_map/ppermute | solution.py:19
  74.1 1.5 collective-permute-done.5
  76.6 1.3 collective-permute-start.6
  77.9 4.9 collective-permute-start.7
  82.8 2.6 collective-permute-done.6
  85.4 1.5 collective-permute-done.7
  86.9 24.7 %fusion.87 = f32[16,16,32,256]{3,0,2,1:T(8,128)} fusion(f32[16,16,32,256]{3,0,2,1:T(8,128)} %fusion.81, f32[16,1,32,256]{3,0,2,1:T(8,128)S(1)} %collective-permute-done.4, f32[16,1,32,256]{3,0,2,1:T(8,128)S(1)} %collective-permute-done.5, f32[16,18,1,256]{3,0,2,1:T(8,128)S(1)} %collective-permute-done.7, f32[16,18,1,256]{3,0,2,1:T(8,128)S(1)} %collective-permute-done.6, ...), kind=kLoop, calls=%fused_computation.164 | loop fusion | flops 50331648 | bytes 27983884 | tf_op jit(solution)/shard_map/jit(_where)/select_n | solution.py:42
  112.9 1.3 collective-permute-start.8
  114.2 12.9 %collective-permute-start.9 = (f32[16,1,32,256]{3,0,2,1:T(8,128)S(1)}, f32[16,1,32,256]{3,0,2,1:T(8,128)S(1)}, u32[]{:S(2)}, u32[]{:S(2)}) collective-permute-start(f32[16,1,32,256]{3,0,2,1:T(8,128)S(1)} %get-tuple-element.38), channel_id=1, source_target_pairs={{0,4},{4,8},{8,12},{12,16},{16,20},{20,24},{24,28},{1,5},{5,9},{9,... | collective-permute-start | bytes 1572872 | tf_op jit(solution)/shard_map/ppermute | solution.py:19
  127.1 1.5 collective-permute-done.9
  129.7 1.3 collective-permute-start.10
  131.0 4.7 collective-permute-start.11
  135.7 2.7 collective-permute-done.10
  138.5 1.5 collective-permute-done.11
  139.9 24.7 %fusion.86 = f32[16,16,32,256]{3,0,2,1:T(8,128)} fusion(f32[16,16,32,256]{3,0,2,1:T(8,128)} %fusion.87, f32[16,1,32,256]{3,0,2,1:T(8,128)S(1)} %collective-permute-done.8, f32[16,1,32,256]{3,0,2,1:T(8,128)S(1)} %collective-permute-done.9, f32[16,18,1,256]{3,0,2,1:T(8,128)S(1)} %collective-permute-done.11, ...), kind=kLoop, calls=%fused_computation.163 | loop fusion | flops 50331648 | bytes 27983884 | tf_op jit(solution)/shard_map/jit(_where)/select_n | solution.py:42
  165.9 1.3 collective-permute-start.12
  167.2 10.1 %collective-permute-start.13 = (f32[16,1,32,256]{3,0,2,1:T(8,128)S(1)}, f32[16,1,32,256]{3,0,2,1:T(8,128)S(1)}, u32[]{:S(2)}, u32[]{:S(2)}) collective-permute-start(f32[16,1,32,256]{3,0,2,1:T(8,128)S(1)} %get-tuple-element.36), channel_id=1, source_target_pairs={{0,4},{4,8},{8,12},{12,16},{16,20},{20,24},{24,28},{1,5},{5,9},{9,... | collective-permute-start | bytes 1572872 | tf_op jit(solution)/shard_map/ppermute | solution.py:19
  177.3 1.5 collective-permute-done.13
  179.9 1.3 collective-permute-start.14
  181.2 4.8 collective-permute-start.15
  186.0 2.7 collective-permute-done.14
  188.8 1.5 collective-permute-done.15
  190.2 24.1 %fusion.85 = f32[16,16,32,256]{3,0,2,1:T(8,128)S(1)} fusion(f32[16,16,32,256]{3,0,2,1:T(8,128)} %fusion.86, f32[16,1,32,256]{3,0,2,1:T(8,128)S(1)} %collective-permute-done.12, f32[16,1,32,256]{3,0,2,1:T(8,128)S(1)} %collective-permute-done.13, f32[16,18,1,256]{3,0,2,1:T(8,128)S(1)} %collective-permute-done.15, ...), kind=kLoop, calls=%fused_computation.162 | loop fusion | flops 50331648 | bytes 27983884 | tf_op jit(solution)/shard_map/jit(_where)/select_n | solution.py:42
  214.4 1.3 collective-permute-start.16
  215.7 9.8 %collective-permute-start.17 = (f32[16,1,32,256]{3,0,2,1:T(8,128)S(1)}, f32[16,1,32,256]{3,0,2,1:T(8,128)S(1)}, u32[]{:S(2)}, u32[]{:S(2)}) collective-permute-start(f32[16,1,32,256]{3,0,2,1:T(8,128)S(1)} %get-tuple-element.34), channel_id=1, source_target_pairs={{0,4},{4,8},{8,12},{12,16},{16,20},{20,24},{24,28},{1,5},{5,9},{9,... | collective-permute-start | bytes 1572872 | tf_op jit(solution)/shard_map/ppermute | solution.py:19
  225.5 1.5 collective-permute-done.17
  228.4 5.1 collective-permute-start.19
  233.4 2.5 collective-permute-done.18
  236.0 1.5 collective-permute-done.19
  237.4 13.0 %fusion.80 = f32[16,16,32,256]{3,0,2,1:T(8,128)} fusion(f32[16,16,32,256]{3,0,2,1:T(8,128)S(1)} %fusion.85, f32[16,1,32,256]{3,0,2,1:T(8,128)S(1)} %collective-permute-done.16, f32[16,1,32,256]{3,0,2,1:T(8,128)S(1)} %collective-permute-done.17, f32[16,18,1,256]{3,0,2,1:T(8,128)S(1)} %collective-permute-done.19, ...), kind=kLoop, calls=%fused_computation.157 | loop fusion | flops 50331648 | bytes 19595276 | tf_op jit(solution)/shard_map/jit(_where)/select_n | solution.py:42
  253.0 9.8 %collective-permute-start.21 = (f32[16,1,32,256]{3,0,2,1:T(8,128)S(1)}, f32[16,1,32,256]{3,0,2,1:T(8,128)S(1)}, u32[]{:S(2)}, u32[]{:S(2)}) collective-permute-start(f32[16,1,32,256]{3,0,2,1:T(8,128)S(1)} %get-tuple-element.32), channel_id=1, source_target_pairs={{0,4},{4,8},{8,12},{12,16},{16,20},{20,24},{24,28},{1,5},{5,9},{9,... | collective-permute-start | bytes 1572872 | tf_op jit(solution)/shard_map/ppermute | solution.py:19
  262.9 1.5 collective-permute-done.21
  265.4 1.3 collective-permute-start.22
  266.7 4.8 collective-permute-start.23
  271.6 2.7 collective-permute-done.22
  274.3 1.5 collective-permute-done.23
  275.8 22.7 %fusion.84 = f32[16,16,32,256]{3,0,2,1:T(8,128)} fusion(f32[16,16,32,256]{3,0,2,1:T(8,128)S(1)} %fusion.85, f32[16,16,32,256]{3,0,2,1:T(8,128)} %fusion.80, f32[16,1,32,256]{3,0,2,1:T(8,128)S(1)} %collective-permute-done.20, f32[16,1,32,256]{3,0,2,1:T(8,128)S(1)} %collective-permute-done.21, f32[16,18,1,256]{3,0,2,1:T(8,128)S(1)} %collective-permute-done.23, ...), kind=kLoop, calls=%fused_computation.161 | loop fusion | flops 50331648 | bytes 27983884 | tf_op jit(solution)/shard_map/jit(_where)/select_n | solution.py:42
  301.0 11.3 %collective-permute-start.25 = (f32[16,1,32,256]{3,0,2,1:T(8,128)S(1)}, f32[16,1,32,256]{3,0,2,1:T(8,128)S(1)}, u32[]{:S(2)}, u32[]{:S(2)}) collective-permute-start(f32[16,1,32,256]{3,0,2,1:T(8,128)S(1)} %get-tuple-element.30), channel_id=1, source_target_pairs={{0,4},{4,8},{8,12},{12,16},{16,20},{20,24},{24,28},{1,5},{5,9},{9,... | collective-permute-start | bytes 1572872 | tf_op jit(solution)/shard_map/ppermute | solution.py:19
  312.3 1.5 collective-permute-done.25
  316.2 4.7 collective-permute-start.27
  321.6 2.1 collective-permute-done.26
  323.7 1.5 collective-permute-done.27
  325.1 22.7 %fusion.83 = f32[16,16,32,256]{3,0,2,1:T(8,128)} fusion(f32[16,16,32,256]{3,0,2,1:T(8,128)S(1)} %fusion.85, f32[16,16,32,256]{3,0,2,1:T(8,128)} %fusion.84, f32[16,1,32,256]{3,0,2,1:T(8,128)S(1)} %collective-permute-done.24, f32[16,1,32,256]{3,0,2,1:T(8,128)S(1)} %collective-permute-done.25, f32[16,18,1,256]{3,0,2,1:T(8,128)S(1)} %collective-permute-done.27, ...), kind=kLoop, calls=%fused_computation.160 | loop fusion | flops 50331648 | bytes 27983884 | tf_op jit(solution)/shard_map/jit(_where)/select_n | solution.py:42
  350.4 13.9 %collective-permute-start.29 = (f32[16,1,32,256]{3,0,2,1:T(8,128)S(1)}, f32[16,1,32,256]{3,0,2,1:T(8,128)S(1)}, u32[]{:S(2)}, u32[]{:S(2)}) collective-permute-start(f32[16,1,32,256]{3,0,2,1:T(8,128)S(1)} %get-tuple-element.28), channel_id=1, source_target_pairs={{0,4},{4,8},{8,12},{12,16},{16,20},{20,24},{24,28},{1,5},{5,9},{9,... | collective-permute-start | bytes 1572872 | tf_op jit(solution)/shard_map/ppermute | solution.py:19
  368.2 4.7 collective-permute-start.31
  373.0 2.7 collective-permute-done.30
  375.7 1.5 collective-permute-done.31
  377.2 22.6 %fusion.82 = f32[16,16,32,256]{3,0,2,1:T(8,128)} fusion(f32[16,16,32,256]{3,0,2,1:T(8,128)S(1)} %fusion.85, f32[16,16,32,256]{3,0,2,1:T(8,128)} %fusion.83, f32[16,1,32,256]{3,0,2,1:T(8,128)S(1)} %collective-permute-done.28, f32[16,1,32,256]{3,0,2,1:T(8,128)S(1)} %collective-permute-done.29, f32[16,18,1,256]{3,0,2,1:T(8,128)S(1)} %collective-permute-done.31, ...), kind=kLoop, calls=%fused_computation.159 | loop fusion | flops 50331648 | bytes 27983884 | tf_op jit(solution)/shard_map/jit(_where)/select_n | solution.py:42
  399.8 32.9 %copy.61 = f32[16,16,32,256]{0,3,2,1:T(8,128)} copy(f32[16,16,32,256]{3,0,2,1:T(8,128)} %fusion.82) | data formatting | bytes 16777216 | tf_op jit(solution)/shard_map/jit(_where)/select_n | solution.py:42
  432.7 1.8 gather_fusion
  435.5 39.7 %all-to-all-start = ((f32[32,1,128]{2,1,0:T(1,128)}), f32[32,1,128]{2,1,0:T(1,128)S(1)}, u32[]{:S(2)}, u32[]{:S(2)}) async-start(f32[32,1,128]{2,1,0:T(1,128)} %reshape.93), calls=%async_computation | async-start | bytes 32768 | tf_op jit(solution)/shard_map/all_to_all | solution.py:74
  475.2 11.6 %copy.66 = f32[16,16,32,256]{3,2,1,0:T(8,128)} copy(f32[16,16,32,256]{3,0,2,1:T(8,128)} %fusion.82) | data formatting | bytes 16777216
  488.7 12.2 %psum.14 = f32[16,16]{1,0:T(8,128)S(1)} all-reduce(f32[16,16]{1,0:T(8,128)S(1)} %fusion.109), channel_id=1, replica_groups=mesh['gx'=8,'gy'=4] {'gy'}, use_global_device_ids=true, to_apply=%region_1.2 | all-reduce | flops 256 | bytes 2048 | tf_op jit(solution)/shard_map/psum | solution.py:82
  500.9 12.7 %psum.15 = f32[16,16]{1,0:T(8,128)} all-reduce(f32[16,16]{1,0:T(8,128)S(1)} %psum.14), channel_id=1, replica_groups=mesh['gx'=8,'gy'=4] {'gx'}, use_global_device_ids=true, to_apply=%region_2.3 | all-reduce | flops 256 | bytes 2048 | tf_op jit(solution)/shard_map/psum | solution.py:81
  (69 shorter events, 29.8 us)
Async XLA Ops:
  0.6 15.4 %copy-start = (f32[16,16,32,256]{3,2,1,0:T(8,128)S(1)}, f32[16,16,32,256]{3,2,1,0:T(8,128)}, u32[]{:S(2)}) copy-start(f32[16,16,32,256]{3,2,1,0:T(8,128)} %param.7) | copy-start | bytes 25165828
  0.6 14.4 %copy-start.1 = (f32[16,32,256]{2,1,0:T(8,128)S(1)}, f32[16,32,256]{2,1,0:T(8,128)}, u32[]{:S(2)}) copy-start(f32[16,32,256]{2,1,0:T(8,128)} %param.8) | copy-start | bytes 1572868
  10.7 15.3 %copy-start.2 = (f32[16,16,32,256]{3,0,2,1:T(8,128)}, f32[16,16,32,256]{3,0,2,1:T(8,128)S(1)}, u32[]{:S(2)}) copy-start(f32[16,16,32,256]{3,0,2,1:T(8,128)S(1)} %copy.60) | copy-start | bytes 25165828
  10.8 4.4 collective-permute-start.1
  13.3 12.8 %collective-permute-start = (f32[16,1,32,256]{3,0,2,1:T(8,128)S(1)}, f32[16,1,32,256]{3,0,2,1:T(8,128)S(1)}, u32[]{:S(2)}, u32[]{:S(2)}) collective-permute-start(f32[16,1,32,256]{3,0,2,1:T(8,128)S(1)} %get-tuple-element.42), channel_id=1, source_target_pairs={{4,0},{8,4},{12,8},{16,12},{20,16},{24,20},{28,24},{5,1},{9,5},{13... | collective-permute-start | bytes 1572872 | tf_op jit(solution)/shard_map/ppermute | solution.py:21
  16.0 18.2 %copy-start.5 = (f32[3]{0:T(128)S(1)}, f32[3]{0:T(128)}, u32[]{:S(2)}) copy-start(f32[3]{0:T(128)} %param.9) | copy-start | bytes 40
  28.0 9.0 %collective-permute-start.2 = (f32[16,18,1,256]{3,0,2,1:T(8,128)S(1)}, f32[16,18,1,256]{3,0,2,1:T(8,128)S(1)}, u32[]{:S(2)}, u32[]{:S(2)}) collective-permute-start(f32[16,18,1,256]{3,0,2,1:T(8,128)S(1)} %get-tuple-element.26), channel_id=1, source_target_pairs={{1,0},{2,1},{3,2},{5,4},{6,5},{7,6},{9,8},{10,9},{11,10},{13,12},{... | collective-permute-start | bytes 884744 | tf_op jit(solution)/shard_map/ppermute | solution.py:21
  29.3 9.2 %collective-permute-start.3 = (f32[16,18,1,256]{3,0,2,1:T(8,128)S(1)}, f32[16,18,1,256]{3,0,2,1:T(8,128)S(1)}, u32[]{:S(2)}, u32[]{:S(2)}) collective-permute-start(f32[16,18,1,256]{3,0,2,1:T(8,128)S(1)} %get-tuple-element.27), channel_id=1, source_target_pairs={{0,1},{1,2},{2,3},{4,5},{5,6},{6,7},{8,9},{9,10},{10,11},{12,13},{... | collective-permute-start | bytes 884744 | tf_op jit(solution)/shard_map/ppermute | solution.py:19
  65.0 9.1 %collective-permute-start.4 = (f32[16,1,32,256]{3,0,2,1:T(8,128)S(1)}, f32[16,1,32,256]{3,0,2,1:T(8,128)S(1)}, u32[]{:S(2)}, u32[]{:S(2)}) collective-permute-start(f32[16,1,32,256]{3,0,2,1:T(8,128)S(1)} %get-tuple-element.41), channel_id=1, source_target_pairs={{4,0},{8,4},{12,8},{16,12},{20,16},{24,20},{28,24},{5,1},{9,5},{13... | collective-permute-start | bytes 1572872 | tf_op jit(solution)/shard_map/ppermute | solution.py:21
  66.3 9.3 %collective-permute-start.5 = (f32[16,1,32,256]{3,0,2,1:T(8,128)S(1)}, f32[16,1,32,256]{3,0,2,1:T(8,128)S(1)}, u32[]{:S(2)}, u32[]{:S(2)}) collective-permute-start(f32[16,1,32,256]{3,0,2,1:T(8,128)S(1)} %get-tuple-element.40), channel_id=1, source_target_pairs={{0,4},{4,8},{8,12},{12,16},{16,20},{20,24},{24,28},{1,5},{5,9},{9,... | collective-permute-start | bytes 1572872 | tf_op jit(solution)/shard_map/ppermute | solution.py:19
  76.6 8.8 %collective-permute-start.6 = (f32[16,18,1,256]{3,0,2,1:T(8,128)S(1)}, f32[16,18,1,256]{3,0,2,1:T(8,128)S(1)}, u32[]{:S(2)}, u32[]{:S(2)}) collective-permute-start(f32[16,18,1,256]{3,0,2,1:T(8,128)S(1)} %get-tuple-element.24), channel_id=1, source_target_pairs={{1,0},{2,1},{3,2},{5,4},{6,5},{7,6},{9,8},{10,9},{11,10},{13,12},{... | collective-permute-start | bytes 884744 | tf_op jit(solution)/shard_map/ppermute | solution.py:21
  77.9 8.9 %collective-permute-start.7 = (f32[16,18,1,256]{3,0,2,1:T(8,128)S(1)}, f32[16,18,1,256]{3,0,2,1:T(8,128)S(1)}, u32[]{:S(2)}, u32[]{:S(2)}) collective-permute-start(f32[16,18,1,256]{3,0,2,1:T(8,128)S(1)} %get-tuple-element.25), channel_id=1, source_target_pairs={{0,1},{1,2},{2,3},{4,5},{5,6},{6,7},{8,9},{9,10},{10,11},{12,13},{... | collective-permute-start | bytes 884744 | tf_op jit(solution)/shard_map/ppermute | solution.py:19
  112.9 14.2 %collective-permute-start.8 = (f32[16,1,32,256]{3,0,2,1:T(8,128)S(1)}, f32[16,1,32,256]{3,0,2,1:T(8,128)S(1)}, u32[]{:S(2)}, u32[]{:S(2)}) collective-permute-start(f32[16,1,32,256]{3,0,2,1:T(8,128)S(1)} %get-tuple-element.39), channel_id=1, source_target_pairs={{4,0},{8,4},{12,8},{16,12},{20,16},{24,20},{28,24},{5,1},{9,5},{13... | collective-permute-start | bytes 1572872 | tf_op jit(solution)/shard_map/ppermute | solution.py:21
  114.2 14.4 %collective-permute-start.9 = (f32[16,1,32,256]{3,0,2,1:T(8,128)S(1)}, f32[16,1,32,256]{3,0,2,1:T(8,128)S(1)}, u32[]{:S(2)}, u32[]{:S(2)}) collective-permute-start(f32[16,1,32,256]{3,0,2,1:T(8,128)S(1)} %get-tuple-element.38), channel_id=1, source_target_pairs={{0,4},{4,8},{8,12},{12,16},{16,20},{20,24},{24,28},{1,5},{5,9},{9,... | collective-permute-start | bytes 1572872 | tf_op jit(solution)/shard_map/ppermute | solution.py:19
  129.7 8.8 %collective-permute-start.10 = (f32[16,18,1,256]{3,0,2,1:T(8,128)S(1)}, f32[16,18,1,256]{3,0,2,1:T(8,128)S(1)}, u32[]{:S(2)}, u32[]{:S(2)}) collective-permute-start(f32[16,18,1,256]{3,0,2,1:T(8,128)S(1)} %get-tuple-element.22), channel_id=1, source_target_pairs={{1,0},{2,1},{3,2},{5,4},{6,5},{7,6},{9,8},{10,9},{11,10},{13,12},{... | collective-permute-start | bytes 884744 | tf_op jit(solution)/shard_map/ppermute | solution.py:21
  131.0 8.9 %collective-permute-start.11 = (f32[16,18,1,256]{3,0,2,1:T(8,128)S(1)}, f32[16,18,1,256]{3,0,2,1:T(8,128)S(1)}, u32[]{:S(2)}, u32[]{:S(2)}) collective-permute-start(f32[16,18,1,256]{3,0,2,1:T(8,128)S(1)} %get-tuple-element.23), channel_id=1, source_target_pairs={{0,1},{1,2},{2,3},{4,5},{5,6},{6,7},{8,9},{9,10},{10,11},{12,13},{... | collective-permute-start | bytes 884744 | tf_op jit(solution)/shard_map/ppermute | solution.py:19
  165.9 11.4 %collective-permute-start.12 = (f32[16,1,32,256]{3,0,2,1:T(8,128)S(1)}, f32[16,1,32,256]{3,0,2,1:T(8,128)S(1)}, u32[]{:S(2)}, u32[]{:S(2)}) collective-permute-start(f32[16,1,32,256]{3,0,2,1:T(8,128)S(1)} %get-tuple-element.37), channel_id=1, source_target_pairs={{4,0},{8,4},{12,8},{16,12},{20,16},{24,20},{28,24},{5,1},{9,5},{13... | collective-permute-start | bytes 1572872 | tf_op jit(solution)/shard_map/ppermute | solution.py:21
  167.2 11.6 %collective-permute-start.13 = (f32[16,1,32,256]{3,0,2,1:T(8,128)S(1)}, f32[16,1,32,256]{3,0,2,1:T(8,128)S(1)}, u32[]{:S(2)}, u32[]{:S(2)}) collective-permute-start(f32[16,1,32,256]{3,0,2,1:T(8,128)S(1)} %get-tuple-element.36), channel_id=1, source_target_pairs={{0,4},{4,8},{8,12},{12,16},{16,20},{20,24},{24,28},{1,5},{5,9},{9,... | collective-permute-start | bytes 1572872 | tf_op jit(solution)/shard_map/ppermute | solution.py:19
  179.9 8.9 %collective-permute-start.14 = (f32[16,18,1,256]{3,0,2,1:T(8,128)S(1)}, f32[16,18,1,256]{3,0,2,1:T(8,128)S(1)}, u32[]{:S(2)}, u32[]{:S(2)}) collective-permute-start(f32[16,18,1,256]{3,0,2,1:T(8,128)S(1)} %get-tuple-element.20), channel_id=1, source_target_pairs={{1,0},{2,1},{3,2},{5,4},{6,5},{7,6},{9,8},{10,9},{11,10},{13,12},{... | collective-permute-start | bytes 884744 | tf_op jit(solution)/shard_map/ppermute | solution.py:21
  181.2 9.1 %collective-permute-start.15 = (f32[16,18,1,256]{3,0,2,1:T(8,128)S(1)}, f32[16,18,1,256]{3,0,2,1:T(8,128)S(1)}, u32[]{:S(2)}, u32[]{:S(2)}) collective-permute-start(f32[16,18,1,256]{3,0,2,1:T(8,128)S(1)} %get-tuple-element.21), channel_id=1, source_target_pairs={{0,1},{1,2},{2,3},{4,5},{5,6},{6,7},{8,9},{9,10},{10,11},{12,13},{... | collective-permute-start | bytes 884744 | tf_op jit(solution)/shard_map/ppermute | solution.py:19
  214.4 11.1 %collective-permute-start.16 = (f32[16,1,32,256]{3,0,2,1:T(8,128)S(1)}, f32[16,1,32,256]{3,0,2,1:T(8,128)S(1)}, u32[]{:S(2)}, u32[]{:S(2)}) collective-permute-start(f32[16,1,32,256]{3,0,2,1:T(8,128)S(1)} %get-tuple-element.35), channel_id=1, source_target_pairs={{4,0},{8,4},{12,8},{16,12},{20,16},{24,20},{28,24},{5,1},{9,5},{13... | collective-permute-start | bytes 1572872 | tf_op jit(solution)/shard_map/ppermute | solution.py:21
  215.7 11.3 %collective-permute-start.17 = (f32[16,1,32,256]{3,0,2,1:T(8,128)S(1)}, f32[16,1,32,256]{3,0,2,1:T(8,128)S(1)}, u32[]{:S(2)}, u32[]{:S(2)}) collective-permute-start(f32[16,1,32,256]{3,0,2,1:T(8,128)S(1)} %get-tuple-element.34), channel_id=1, source_target_pairs={{0,4},{4,8},{8,12},{12,16},{16,20},{20,24},{24,28},{1,5},{5,9},{9,... | collective-permute-start | bytes 1572872 | tf_op jit(solution)/shard_map/ppermute | solution.py:19
  227.1 8.9 %collective-permute-start.18 = (f32[16,18,1,256]{3,0,2,1:T(8,128)S(1)}, f32[16,18,1,256]{3,0,2,1:T(8,128)S(1)}, u32[]{:S(2)}, u32[]{:S(2)}) collective-permute-start(f32[16,18,1,256]{3,0,2,1:T(8,128)S(1)} %get-tuple-element.18), channel_id=1, source_target_pairs={{1,0},{2,1},{3,2},{5,4},{6,5},{7,6},{9,8},{10,9},{11,10},{13,12},{... | collective-permute-start | bytes 884744 | tf_op jit(solution)/shard_map/ppermute | solution.py:21
  228.4 9.1 %collective-permute-start.19 = (f32[16,18,1,256]{3,0,2,1:T(8,128)S(1)}, f32[16,18,1,256]{3,0,2,1:T(8,128)S(1)}, u32[]{:S(2)}, u32[]{:S(2)}) collective-permute-start(f32[16,18,1,256]{3,0,2,1:T(8,128)S(1)} %get-tuple-element.19), channel_id=1, source_target_pairs={{0,1},{1,2},{2,3},{4,5},{5,6},{6,7},{8,9},{9,10},{10,11},{12,13},{... | collective-permute-start | bytes 884744 | tf_op jit(solution)/shard_map/ppermute | solution.py:19
  251.7 11.1 %collective-permute-start.20 = (f32[16,1,32,256]{3,0,2,1:T(8,128)S(1)}, f32[16,1,32,256]{3,0,2,1:T(8,128)S(1)}, u32[]{:S(2)}, u32[]{:S(2)}) collective-permute-start(f32[16,1,32,256]{3,0,2,1:T(8,128)S(1)} %get-tuple-element.33), channel_id=1, source_target_pairs={{4,0},{8,4},{12,8},{16,12},{20,16},{24,20},{28,24},{5,1},{9,5},{13... | collective-permute-start | bytes 1572872 | tf_op jit(solution)/shard_map/ppermute | solution.py:21
  253.0 11.3 %collective-permute-start.21 = (f32[16,1,32,256]{3,0,2,1:T(8,128)S(1)}, f32[16,1,32,256]{3,0,2,1:T(8,128)S(1)}, u32[]{:S(2)}, u32[]{:S(2)}) collective-permute-start(f32[16,1,32,256]{3,0,2,1:T(8,128)S(1)} %get-tuple-element.32), channel_id=1, source_target_pairs={{0,4},{4,8},{8,12},{12,16},{16,20},{20,24},{24,28},{1,5},{5,9},{9,... | collective-permute-start | bytes 1572872 | tf_op jit(solution)/shard_map/ppermute | solution.py:19
  265.4 8.9 %collective-permute-start.22 = (f32[16,18,1,256]{3,0,2,1:T(8,128)S(1)}, f32[16,18,1,256]{3,0,2,1:T(8,128)S(1)}, u32[]{:S(2)}, u32[]{:S(2)}) collective-permute-start(f32[16,18,1,256]{3,0,2,1:T(8,128)S(1)} %get-tuple-element.16), channel_id=1, source_target_pairs={{1,0},{2,1},{3,2},{5,4},{6,5},{7,6},{9,8},{10,9},{11,10},{13,12},{... | collective-permute-start | bytes 884744 | tf_op jit(solution)/shard_map/ppermute | solution.py:21
  266.7 9.1 %collective-permute-start.23 = (f32[16,18,1,256]{3,0,2,1:T(8,128)S(1)}, f32[16,18,1,256]{3,0,2,1:T(8,128)S(1)}, u32[]{:S(2)}, u32[]{:S(2)}) collective-permute-start(f32[16,18,1,256]{3,0,2,1:T(8,128)S(1)} %get-tuple-element.17), channel_id=1, source_target_pairs={{0,1},{1,2},{2,3},{4,5},{5,6},{6,7},{8,9},{9,10},{10,11},{12,13},{... | collective-permute-start | bytes 884744 | tf_op jit(solution)/shard_map/ppermute | solution.py:19
  299.7 12.6 %collective-permute-start.24 = (f32[16,1,32,256]{3,0,2,1:T(8,128)S(1)}, f32[16,1,32,256]{3,0,2,1:T(8,128)S(1)}, u32[]{:S(2)}, u32[]{:S(2)}) collective-permute-start(f32[16,1,32,256]{3,0,2,1:T(8,128)S(1)} %get-tuple-element.31), channel_id=1, source_target_pairs={{4,0},{8,4},{12,8},{16,12},{20,16},{24,20},{28,24},{5,1},{9,5},{13... | collective-permute-start | bytes 1572872 | tf_op jit(solution)/shard_map/ppermute | solution.py:21
  301.0 12.8 %collective-permute-start.25 = (f32[16,1,32,256]{3,0,2,1:T(8,128)S(1)}, f32[16,1,32,256]{3,0,2,1:T(8,128)S(1)}, u32[]{:S(2)}, u32[]{:S(2)}) collective-permute-start(f32[16,1,32,256]{3,0,2,1:T(8,128)S(1)} %get-tuple-element.30), channel_id=1, source_target_pairs={{0,4},{4,8},{8,12},{12,16},{16,20},{20,24},{24,28},{1,5},{5,9},{9,... | collective-permute-start | bytes 1572872 | tf_op jit(solution)/shard_map/ppermute | solution.py:19
  314.9 8.8 %collective-permute-start.26 = (f32[16,18,1,256]{3,0,2,1:T(8,128)S(1)}, f32[16,18,1,256]{3,0,2,1:T(8,128)S(1)}, u32[]{:S(2)}, u32[]{:S(2)}) collective-permute-start(f32[16,18,1,256]{3,0,2,1:T(8,128)S(1)} %get-tuple-element.14), channel_id=1, source_target_pairs={{1,0},{2,1},{3,2},{5,4},{6,5},{7,6},{9,8},{10,9},{11,10},{13,12},{... | collective-permute-start | bytes 884744 | tf_op jit(solution)/shard_map/ppermute | solution.py:21
  316.2 8.9 %collective-permute-start.27 = (f32[16,18,1,256]{3,0,2,1:T(8,128)S(1)}, f32[16,18,1,256]{3,0,2,1:T(8,128)S(1)}, u32[]{:S(2)}, u32[]{:S(2)}) collective-permute-start(f32[16,18,1,256]{3,0,2,1:T(8,128)S(1)} %get-tuple-element.15), channel_id=1, source_target_pairs={{0,1},{1,2},{2,3},{4,5},{5,6},{6,7},{8,9},{9,10},{10,11},{12,13},{... | collective-permute-start | bytes 884744 | tf_op jit(solution)/shard_map/ppermute | solution.py:19
  321.6 42.8 %copy-start.7 = (s32[1,1,128,1]{2,3,1,0:T(1,128)S(1)}, s32[1,1,128,1]{2,3,1,0:T(1,128)}, u32[]{:S(2)}) copy-start(s32[1,1,128,1]{2,3,1,0:T(1,128)} %param.11) | copy-start | bytes 1540
  321.6 42.9 %copy-start.6 = (s32[1,1,128]{2,1,0:T(1,128)S(1)}, s32[1,1,128]{2,1,0:T(1,128)}, u32[]{:S(2)}) copy-start(s32[1,1,128]{2,1,0:T(1,128)} %param.10) | copy-start | bytes 1540
  349.1 15.5 %collective-permute-start.28 = (f32[16,1,32,256]{3,0,2,1:T(8,128)S(1)}, f32[16,1,32,256]{3,0,2,1:T(8,128)S(1)}, u32[]{:S(2)}, u32[]{:S(2)}) collective-permute-start(f32[16,1,32,256]{3,0,2,1:T(8,128)S(1)} %get-tuple-element.29), channel_id=1, source_target_pairs={{4,0},{8,4},{12,8},{16,12},{20,16},{24,20},{28,24},{5,1},{9,5},{13... | collective-permute-start | bytes 1572872 | tf_op jit(solution)/shard_map/ppermute | solution.py:21
  350.4 15.4 %collective-permute-start.29 = (f32[16,1,32,256]{3,0,2,1:T(8,128)S(1)}, f32[16,1,32,256]{3,0,2,1:T(8,128)S(1)}, u32[]{:S(2)}, u32[]{:S(2)}) collective-permute-start(f32[16,1,32,256]{3,0,2,1:T(8,128)S(1)} %get-tuple-element.28), channel_id=1, source_target_pairs={{0,4},{4,8},{8,12},{12,16},{16,20},{20,24},{24,28},{1,5},{5,9},{9,... | collective-permute-start | bytes 1572872 | tf_op jit(solution)/shard_map/ppermute | solution.py:19
  366.9 8.8 %collective-permute-start.30 = (f32[16,18,1,256]{3,0,2,1:T(8,128)S(1)}, f32[16,18,1,256]{3,0,2,1:T(8,128)S(1)}, u32[]{:S(2)}, u32[]{:S(2)}) collective-permute-start(f32[16,18,1,256]{3,0,2,1:T(8,128)S(1)} %get-tuple-element.12), channel_id=1, source_target_pairs={{1,0},{2,1},{3,2},{5,4},{6,5},{7,6},{9,8},{10,9},{11,10},{13,12},{... | collective-permute-start | bytes 884744 | tf_op jit(solution)/shard_map/ppermute | solution.py:21
  368.2 8.9 %collective-permute-start.31 = (f32[16,18,1,256]{3,0,2,1:T(8,128)S(1)}, f32[16,18,1,256]{3,0,2,1:T(8,128)S(1)}, u32[]{:S(2)}, u32[]{:S(2)}) collective-permute-start(f32[16,18,1,256]{3,0,2,1:T(8,128)S(1)} %get-tuple-element.13), channel_id=1, source_target_pairs={{0,1},{1,2},{2,3},{4,5},{5,6},{6,7},{8,9},{9,10},{10,11},{12,13},{... | collective-permute-start | bytes 884744 | tf_op jit(solution)/shard_map/ppermute | solution.py:19
  399.8 34.8 %copy-start.4 = (f32[1,1,128,16]{2,3,1,0:T(8,128)S(1)}, f32[1,1,128,16]{2,3,1,0:T(8,128)}, u32[]{:S(2)}) copy-start(f32[1,1,128,16]{2,3,1,0:T(8,128)} %param.13) | copy-start | bytes 24580
  435.5 51.3 %all-to-all-start = ((f32[32,1,128]{2,1,0:T(1,128)}), f32[32,1,128]{2,1,0:T(1,128)S(1)}, u32[]{:S(2)}, u32[]{:S(2)}) async-start(f32[32,1,128]{2,1,0:T(1,128)} %reshape.93), calls=%async_computation | async-start | bytes 32768 | tf_op jit(solution)/shard_map/all_to_all | solution.py:74
  488.4 25.2 %copy-start.3 = (f32[16,16]{1,0:T(8,128)}, f32[16,16]{1,0:T(8,128)S(1)}, u32[]{:S(2)}) copy-start(f32[16,16]{1,0:T(8,128)S(1)} %convolution_bitcast_fusion) | copy-start | bytes 3076
